TPU v7x, 128 devices: a whole 4x4x4 slice. The times are simulated.
128 devices in a mesh: grp: 8 (over z, y_lo), dev: 16 (over x, y_hi, core).
Axes of the slice: x: 4, y: 4 (y_hi: 2, y_lo: 2; y = y_hi * 2 + y_lo), z: 4, core: 2. Of those that a mesh axis runs over, the one named last changes fastest.
Arguments:
- vertex_values: bfloat16 [8192, 128, 256], P(('grp', 'dev')), may hold values from -6 to 6
- position_domain_label: int32 [8192], P(('grp', 'dev')), may hold values from 0 to 64, as said below
- position_vertex_tally: int32 [8192], P(('grp', 'dev')), may hold values from 0 to 128, as said below
- normalizer_gain: float32 [256], replicated, may hold values from 0.1 to 1.9
- embedding_matrix: bfloat16 [256, 256], replicated, may hold values from -0.375 to 0.375
- partition_input_matrix: bfloat16 [256, 256], replicated, may hold values from -0.375 to 0.375
- partition_score_matrix: bfloat16 [32, 64], replicated, may hold values from -60 to 60
- softmax_sharpness: float32 [8], replicated, may hold values from 0.3 to 1
- partition_attention_maps: float32 [3, 32, 32], replicated, may hold values from -10 to 10
- readout_matrix: bfloat16 [256, 256], replicated, may hold values from -1.5 to 1.5
Outputs:
- updated: bfloat16 [8192, 128, 256], P(('grp', 'dev'))
Inputs may be any that keep to these rules, and one draw needn't show every extreme that they name: `position_domain_label`: on each device the used slots come first; a device may use none. Reading the devices in order and their used slots in order lists every mesh's blocks as one run, meshes in increasing order, each mesh 2 or more blocks. Exactly 4096 slots are used in all, and some device uses all 64 of its slots. `position_vertex_tally`: 128 in every used slot except the last block of each mesh, which holds 1 to 128; 0 in unused slots.
All inputs are finite; a program needn't handle non-finite values.
Results may differ from a plain program's by a relative error of at most 0.012.
The roundings to bfloat16 on the way count: a program that leaves them out, or rounds other values in their place, can miss the bound.
Values may be sent and summed in bfloat16 or wider, within the bound.
No kernel may reach another device: no remote copies, remote signals or barrier semaphores. Data moves between devices by JAX's collectives and lax.ppermute only.
A program may use at most 128 MiB of HBM per device.

v0:
```python
import jax
import jax.numpy as jnp
from jax import lax
from jax.sharding import PartitionSpec as P

MESHES = 64


def partition_routine(
    tile_sequence,
    vertex_tallies,
    domain_sequence,
    normalizer_gain,
    embedding_matrix,
    partition_input_matrix,
    partition_score_matrix,
    softmax_sharpness,
):
    tile_amount, tile_height, model_width = tile_sequence.shape
    attention_group_amount = softmax_sharpness.shape[0]
    head_width = model_width // attention_group_amount
    partition_amount = partition_score_matrix.shape[1]
    flattened = tile_sequence.reshape(tile_amount * tile_height, model_width).astype(jnp.float32)
    centre = flattened - jnp.mean(flattened, axis=1, keepdims=True)
    spread = jnp.mean(centre * centre, axis=1, keepdims=True)
    normed = (centre * lax.rsqrt(spread + 1e-05) * normalizer_gain).astype(jnp.bfloat16)
    features = jnp.dot(normed, embedding_matrix, preferred_element_type=jnp.float32).astype(
        jnp.bfloat16
    )
    middles = jnp.dot(normed, partition_input_matrix, preferred_element_type=jnp.float32).astype(
        jnp.bfloat16
    )
    partition_scores = jnp.dot(
        middles.reshape(-1, head_width), partition_score_matrix, preferred_element_type=jnp.float32
    )
    partition_scores = (
        partition_scores.reshape(tile_amount, tile_height, attention_group_amount, partition_amount)
        / softmax_sharpness[:, None]
    )
    living = (
        lax.broadcasted_iota(jnp.int32, (tile_amount, tile_height), 1) < vertex_tallies[:, None]
    ).astype(jnp.float32)
    partition_shares = (
        jax.nn.softmax(partition_scores, axis=-1) * living[:, :, None, None]
    ).astype(jnp.bfloat16)
    partial_sums = jnp.einsum(
        "bphm,bphd->bhmd",
        partition_shares,
        features.reshape(tile_amount, tile_height, attention_group_amount, head_width),
        preferred_element_type=jnp.float32,
    )
    partial_totals = jnp.sum(partition_shares.astype(jnp.float32), axis=1)
    one_hot = (
        domain_sequence[:, None] == lax.broadcasted_iota(jnp.int32, (tile_amount, MESHES), 1)
    ).astype(jnp.float32)
    domain_accumulated = jnp.dot(one_hot.T, partial_sums.reshape(tile_amount, -1))
    domain_share_accumulated = jnp.dot(one_hot.T, partial_totals.reshape(tile_amount, -1))
    return (
        partition_shares.reshape(
            tile_amount, tile_height, attention_group_amount * partition_amount
        ),
        domain_accumulated,
        domain_share_accumulated,
    )


def attend_tokens(domain_accumulated, domain_share_accumulated, partition_attention_maps):
    row_count, partition_amount = domain_share_accumulated.shape
    head_width = partition_attention_maps.shape[1]
    tokens = domain_accumulated.reshape(row_count, partition_amount, head_width) / (
        domain_share_accumulated[:, :, None] + 1.0
    )
    queries = jnp.einsum("rmd,de->rme", tokens, partition_attention_maps[0])
    key_rows = jnp.einsum("rmd,de->rme", tokens, partition_attention_maps[1])
    values = jnp.einsum("rmd,de->rme", tokens, partition_attention_maps[2])
    scores = jnp.einsum("rme,rne->rmn", queries, key_rows) * head_width ** (-0.5)
    token_probs = jax.nn.softmax(scores, axis=-1)
    blended = jnp.einsum("rmn,rne->rme", token_probs, values)
    return blended.reshape(row_count, partition_amount * head_width).astype(jnp.bfloat16)


def spread_phase(
    tile_sequence, vertex_tallies, domain_sequence, partition_shares, tokens, readout_matrix
):
    tile_amount, tile_height, model_width = tile_sequence.shape
    attention_group_amount = tokens.shape[0] // MESHES
    partition_amount = partition_shares.shape[2] // attention_group_amount
    head_width = model_width // attention_group_amount
    tables = tokens.reshape(MESHES, attention_group_amount, partition_amount, head_width)
    chosen = jnp.take(tables, jnp.minimum(domain_sequence, MESHES - 1), axis=0)
    blended = jnp.einsum(
        "bphm,bhmd->bphd",
        partition_shares.reshape(
            tile_amount, tile_height, attention_group_amount, partition_amount
        ),
        chosen,
        preferred_element_type=jnp.float32,
    ).astype(jnp.bfloat16)
    projected = jnp.dot(
        blended.reshape(-1, model_width), readout_matrix, preferred_element_type=jnp.float32
    )
    living = (
        lax.broadcasted_iota(jnp.int32, (tile_amount, tile_height), 1) < vertex_tallies[:, None]
    ).astype(jnp.float32)
    result = (
        tile_sequence.reshape(-1, model_width).astype(jnp.float32) + projected
    ) * living.reshape(-1, 1)
    return result.reshape(tile_amount, tile_height, model_width).astype(jnp.bfloat16)


def on_device(
    vertex_values,
    position_domain_label,
    position_vertex_tally,
    normalizer_gain,
    embedding_matrix,
    partition_input_matrix,
    partition_score_matrix,
    softmax_sharpness,
    partition_attention_maps,
    readout_matrix,
):
    slot_total, tile_height, model_width = vertex_values.shape
    attention_group_amount = softmax_sharpness.shape[0]
    partition_amount = partition_score_matrix.shape[1]
    group_count = slot_total // 16
    grouped = (
        vertex_values.reshape(group_count, 16, tile_height, model_width),
        position_vertex_tally.reshape(group_count, 16),
        position_domain_label.reshape(group_count, 16),
    )

    def gather_step(running, lookup_element):
        partition_shares, domain_accumulated, domain_share_accumulated = partition_routine(
            lookup_element[0],
            lookup_element[1],
            lookup_element[2],
            normalizer_gain,
            embedding_matrix,
            partition_input_matrix,
            partition_score_matrix,
            softmax_sharpness,
        )
        return (
            (running[0] + domain_accumulated, running[1] + domain_share_accumulated),
            partition_shares,
        )

    initial = (
        jnp.zeros((MESHES, model_width * partition_amount), jnp.float32),
        jnp.zeros((MESHES, attention_group_amount * partition_amount), jnp.float32),
    )
    (domain_accumulated, domain_share_accumulated), partition_shares = lax.scan(
        gather_step, initial, grouped
    )
    whole_sums, whole_totals = lax.psum(
        (
            domain_accumulated.reshape(MESHES * attention_group_amount, -1),
            domain_share_accumulated.reshape(MESHES * attention_group_amount, -1),
        ),
        ("grp", "dev"),
    )
    tokens = attend_tokens(whole_sums, whole_totals, partition_attention_maps)

    def spread_step(lookup_element):
        return spread_phase(
            lookup_element[0],
            lookup_element[1],
            lookup_element[2],
            lookup_element[3],
            tokens,
            readout_matrix,
        )

    return lax.map(spread_step, grouped + (partition_shares,)).reshape(vertex_values.shape)


def solution(mesh):
    return jax.shard_map(
        on_device,
        mesh=mesh,
        in_specs=(
            P(("grp", "dev"), None, None),
            P(("grp", "dev")),
            P(("grp", "dev")),
            P(),
            P(),
            P(),
            P(),
            P(),
            P(),
            P(),
        ),
        out_specs=P(("grp", "dev"), None, None),
        check_vma=False,
    )
```

profile of v0, /device:TPU:1, one launch (start us, length us, event | category | flops | bytes accessed | tf_op | source)
XLA Modules:
  0.0 490.3 jit_solution(10821527517631763876)
XLA Ops:
  8.0 115.3 %while.26 = (s32[]{:T(128)}, f32[64,16384]{1,0:T(8,128)}, f32[64,512]{1,0:T(8,128)S(1)}, bf16[4,16,128,512]{2,3,1,0:T(8,128)(2,1)}, s32[4,16]{1,0:T(4,128)S(1)},...) while((s32[]{:T(128)}, f32[64,16384]{1,0:T(8,128)}, ...), condition=%wide.region_6.7_spmd.clone, body=%wide.region_0.6_spmd.clone.sunk | while | flops 723058752 | bytes 48028012 | solution.py:153
  9.6 1.9 multiply_reduce_fusion.3
  11.6 1.8 fusion.110
  14.7 3.6 fusion.111
  18.4 3.4 convert_reduce_fusion.5
  24.9 2.1 fusion.112
  27.0 3.5 reshape.222
  30.5 2.8 convolution_add_fusion.5
  35.2 1.6 convert_reduce_fusion.4
  36.9 1.9 multiply_reduce_fusion.3
  38.8 1.8 fusion.110
  41.9 3.6 fusion.111
  45.6 3.4 convert_reduce_fusion.5
  52.1 2.1 fusion.112
  54.2 3.5 reshape.222
  57.7 5.0 %convolution_add_fusion.5 = f32[64,16384]{1,0:T(8,128)} fusion(bf16[16,16384]{1,0:T(8,128)(2,1)S(1)} %reshape.222, f32[64,16384]{1,0:T(8,128)} %get-tuple-element.383, pred[]{:T(512)S(6)} %compare.3, s32[16]{0:T(128)S(1)} %get-tuple-element.366), kind=kOutput, calls=%fused_computation.27.clone.1 | convolution fusion | flops 35652608 | bytes 8912961 | tf_op jit(solution)/shard_map/while/body/eval_jaxpr/dot_general | solution.py:56
  66.2 1.9 multiply_reduce_fusion.3
  68.1 1.8 fusion.110
  71.3 3.6 fusion.111
  74.9 3.4 convert_reduce_fusion.5
  81.5 2.1 fusion.112
  83.5 3.5 reshape.222
  87.0 5.0 %convolution_add_fusion.5 = f32[64,16384]{1,0:T(8,128)} fusion(bf16[16,16384]{1,0:T(8,128)(2,1)S(1)} %reshape.222, f32[64,16384]{1,0:T(8,128)} %get-tuple-element.383, pred[]{:T(512)S(6)} %compare.3, s32[16]{0:T(128)S(1)} %get-tuple-element.366), kind=kOutput, calls=%fused_computation.27.clone.1 | convolution fusion | flops 35652608 | bytes 8912961 | tf_op jit(solution)/shard_map/while/body/eval_jaxpr/dot_general | solution.py:56
  95.6 1.9 multiply_reduce_fusion.3
  97.5 1.8 fusion.110
  100.6 3.6 fusion.111
  104.3 3.4 convert_reduce_fusion.5
  110.8 2.1 fusion.112
  112.9 3.5 reshape.222
  116.4 5.0 %convolution_add_fusion.5 = f32[64,16384]{1,0:T(8,128)} fusion(bf16[16,16384]{1,0:T(8,128)(2,1)S(1)} %reshape.222, f32[64,16384]{1,0:T(8,128)} %get-tuple-element.383, pred[]{:T(512)S(6)} %compare.3, s32[16]{0:T(128)S(1)} %get-tuple-element.366), kind=kOutput, calls=%fused_computation.27.clone.1 | convolution fusion | flops 35652608 | bytes 8912961 | tf_op jit(solution)/shard_map/while/body/eval_jaxpr/dot_general | solution.py:56
  123.3 5.0 %reshape.192 = f32[512,2048]{1,0:T(8,128)} reshape(f32[64,16384]{1,0:T(8,128)} %get-tuple-element.111) | data formatting | bytes 8388608 | tf_op jit(solution)/shard_map/reshape | solution.py:158
  129.2 157.6 %all-reduce.3.cloned.1.call-done = (f32[512,2048]{1,0:T(8,128)}, f32[512,64]{0,1:T(8,128)}) async-done(((f32[512,2048]{1,0:T(8,128)}, f32[512,64]{0,1:T(8,128)}), (f32[512,2048]{1,0:T(8,128)}, f32[512,64]{0,1:T(8,128)})) %all-reduce.3.cloned.1.call-update) | async-done | bytes 4325392 | tf_op jit(solution)/shard_map/psum | solution.py:156
  287.8 2.5 div.47
  290.3 5.4 %copy.52 = f32[512,2048]{1,0:T(8,128)} copy(f32[512,2048]{0,1:T(8,128)} %bitcast.167) | data formatting | bytes 8388608 | tf_op jit(solution)/shard_map/div | solution.py:70
  295.7 5.7 %div.49 = bf16[512,2048]{1,0:T(8,128)(2,1)} divide(f32[512,2048]{1,0:T(8,128)} %get-tuple-element.218, f32[512,2048]{1,0:T(8,128)} %copy.52) | non-fusion elementwise | flops 1048576 | bytes 10485760 | tf_op jit(solution)/shard_map/div | solution.py:70
  301.3 3.0 copy.53
  304.4 2.1 fusion.39
  306.5 2.0 fusion.37
  308.5 2.1 fusion.35
  310.6 8.8 %copy.56 = bf16[512,64,32]{1,2,0:T(8,128)(2,1)} copy(bf16[512,64,32]{0,2,1:T(8,128)(2,1)} %fusion.39) | data formatting | bytes 4194304 | tf_op jit(solution)/shard_map/rmd,de->rme/dot_general | solution.py:73
  319.3 8.9 %copy.57 = bf16[512,64,32]{1,2,0:T(8,128)(2,1)} copy(bf16[512,64,32]{0,2,1:T(8,128)(2,1)} %fusion.37) | data formatting | bytes 4194304 | tf_op jit(solution)/shard_map/rmd,de->rme/dot_general | solution.py:74
  328.3 7.9 %copy.60 = bf16[512,64,32]{1,2,0:T(8,128)(2,1)} copy(bf16[512,64,32]{0,2,1:T(8,128)(2,1)S(1)} %copy-done) | data formatting | bytes 4194304 | tf_op jit(solution)/shard_map/rmd,de->rme/dot_general | solution.py:75
  336.1 12.5 %multiply_reduce_fusion.1 = (f32[512,64]{1,0:T(8,128)S(1)}, f32[512,64,64]{1,2,0:T(8,128)}) fusion(bf16[512,64,32]{1,2,0:T(8,128)(2,1)} %copy.56, bf16[512,64,32]{1,2,0:T(8,128)(2,1)} %copy.57), kind=kOutput, calls=%fused_computation.61 | convolution fusion | flops 138379264 | bytes 12713984 | tf_op jit(solution)/shard_map/rme,rne->rmn/dot_general | solution.py:76
  348.7 10.3 %fusion.28 = f32[512,64]{1,0:T(8,128)S(1)} fusion(f32[512,64,64]{1,2,0:T(8,128)} %get-tuple-element.229, f32[512,64]{1,0:T(8,128)S(1)} %get-tuple-element.228), kind=kLoop, calls=%fused_computation.62 | loop fusion | flops 6258688 | bytes 8650752 | tf_op jit(solution)/shard_map/reduce_sum | solution.py:77
  359.0 10.4 %fusion.32 = bf16[512,64,32]{1,2,0:T(8,128)(2,1)} fusion(bf16[512,64,32]{1,2,0:T(8,128)(2,1)} %copy.60, f32[512,64,64]{1,2,0:T(8,128)} %get-tuple-element.229, f32[512,64]{1,0:T(8,128)S(1)} %fusion.28, f32[512,64]{1,0:T(8,128)S(1)} %get-tuple-element.228), kind=kOutput, calls=%fused_computation.66 | convolution fusion | flops 140509184 | bytes 12845056 | tf_op jit(solution)/shard_map/rmn,rne->rme/dot_general | solution.py:78
  369.4 6.9 %copy.61 = bf16[512,64,32]{0,2,1:T(8,128)(2,1)} copy(bf16[512,64,32]{1,2,0:T(8,128)(2,1)} %fusion.32) | data formatting | bytes 4194304 | tf_op jit(solution)/shard_map/convert_element_type | solution.py:79
  376.3 2.9 copy.62
  379.3 104.2 %while.25 = (s32[]{:T(128)}, bf16[4,16,128,256]{3,2,1,0:T(8,128)(2,1)}, bf16[4,16,128,256]{3,2,1,0:T(8,128)(2,1)}, s32[4,16]{1,0:T(4,128)S(1)}, bf16[512,2048]{1...) while((s32[]{:T(128)}, ...), condition=%wide.region_12.13_spmd, body=%wide.region_11.12_spmd.sunk | while | flops 338433216 | bytes 26891408 | solution.py:175
  379.6 8.0 %reshape.221 = bf16[64,8,64,32]{3,2,1,0:T(8,128)(2,1)} reshape(bf16[512,2048]{1,0:T(8,128)(2,1)S(1)} %get-tuple-element.432) | data formatting | bytes 4194304 | tf_op jit(solution)/shard_map/while/body/eval_jaxpr/reshape | solution.py:89
  387.6 8.6 %copy.92 = bf16[64,8,64,32]{2,3,1,0:T(8,128)(2,1)} copy(bf16[64,8,64,32]{3,2,1,0:T(8,128)(2,1)} %reshape.221) | data formatting | bytes 4194304 | tf_op jit(solution)/shard_map/while/body/eval_jaxpr/reshape | solution.py:89
  396.2 2.9 gather_fusion
  399.1 1.8 constant_dynamic-slice_fusion.9
  405.6 8.0 %reshape.221 = bf16[64,8,64,32]{3,2,1,0:T(8,128)(2,1)} reshape(bf16[512,2048]{1,0:T(8,128)(2,1)S(1)} %get-tuple-element.432) | data formatting | bytes 4194304 | tf_op jit(solution)/shard_map/while/body/eval_jaxpr/reshape | solution.py:89
  413.6 8.6 %copy.92 = bf16[64,8,64,32]{2,3,1,0:T(8,128)(2,1)} copy(bf16[64,8,64,32]{3,2,1,0:T(8,128)(2,1)} %reshape.221) | data formatting | bytes 4194304 | tf_op jit(solution)/shard_map/while/body/eval_jaxpr/reshape | solution.py:89
  422.2 2.9 gather_fusion
  425.1 1.8 constant_dynamic-slice_fusion.9
  431.5 8.0 %reshape.221 = bf16[64,8,64,32]{3,2,1,0:T(8,128)(2,1)} reshape(bf16[512,2048]{1,0:T(8,128)(2,1)S(1)} %get-tuple-element.432) | data formatting | bytes 4194304 | tf_op jit(solution)/shard_map/while/body/eval_jaxpr/reshape | solution.py:89
  439.6 8.6 %copy.92 = bf16[64,8,64,32]{2,3,1,0:T(8,128)(2,1)} copy(bf16[64,8,64,32]{3,2,1,0:T(8,128)(2,1)} %reshape.221) | data formatting | bytes 4194304 | tf_op jit(solution)/shard_map/while/body/eval_jaxpr/reshape | solution.py:89
  448.2 2.9 gather_fusion
  451.1 1.8 constant_dynamic-slice_fusion.9
  457.5 8.0 %reshape.221 = bf16[64,8,64,32]{3,2,1,0:T(8,128)(2,1)} reshape(bf16[512,2048]{1,0:T(8,128)(2,1)S(1)} %get-tuple-element.432) | data formatting | bytes 4194304 | tf_op jit(solution)/shard_map/while/body/eval_jaxpr/reshape | solution.py:89
  465.6 8.6 %copy.92 = bf16[64,8,64,32]{2,3,1,0:T(8,128)(2,1)} copy(bf16[64,8,64,32]{3,2,1,0:T(8,128)(2,1)} %reshape.221) | data formatting | bytes 4194304 | tf_op jit(solution)/shard_map/while/body/eval_jaxpr/reshape | solution.py:89
  474.1 2.9 gather_fusion
  477.1 1.8 constant_dynamic-slice_fusion.9
  (144 shorter events, 52.2 us)
Async XLA Ops:
  6.5 280.3 %all-reduce.3.cloned.1.call-start = ((), (), s32[]{:S(2)}) async-start(), calls=%async_computation | async-start | bytes 8650752 | tf_op jit(solution)/shard_map/psum | solution.py:156
  8.0 5.3 %copy-start.1 = (bf16[256,256]{1,0:T(8,128)(2,1)S(1)}, bf16[256,256]{1,0:T(8,128)(2,1)}, u32[]{:S(2)}) copy-start(bf16[256,256]{1,0:T(8,128)(2,1)} %get-tuple-element.403) | copy-start | bytes 393220 | tf_op jit(solution)/shard_map/while
  11.5 3.1 copy-start.5
  11.5 3.1 copy-start.6
  18.3 3.5 copy-start.2
  35.2 5.3 %copy-start.1 = (bf16[256,256]{1,0:T(8,128)(2,1)S(1)}, bf16[256,256]{1,0:T(8,128)(2,1)}, u32[]{:S(2)}) copy-start(bf16[256,256]{1,0:T(8,128)(2,1)} %get-tuple-element.403) | copy-start | bytes 393220 | tf_op jit(solution)/shard_map/while
  38.8 3.1 copy-start.5
  38.8 3.1 copy-start.6
  45.5 3.5 copy-start.2
  64.6 5.3 %copy-start.1 = (bf16[256,256]{1,0:T(8,128)(2,1)S(1)}, bf16[256,256]{1,0:T(8,128)(2,1)}, u32[]{:S(2)}) copy-start(bf16[256,256]{1,0:T(8,128)(2,1)} %get-tuple-element.403) | copy-start | bytes 393220 | tf_op jit(solution)/shard_map/while
  68.1 3.1 copy-start.5
  68.1 3.1 copy-start.6
  74.8 3.5 copy-start.2
  94.0 5.3 %copy-start.1 = (bf16[256,256]{1,0:T(8,128)(2,1)S(1)}, bf16[256,256]{1,0:T(8,128)(2,1)}, u32[]{:S(2)}) copy-start(bf16[256,256]{1,0:T(8,128)(2,1)} %get-tuple-element.403) | copy-start | bytes 393220 | tf_op jit(solution)/shard_map/while
  97.5 3.1 copy-start.5
  97.5 3.1 copy-start.6
  104.2 3.5 copy-start.2
  301.3 3.1 copy-start.3
  319.3 8.9 %copy-start = (bf16[512,64,32]{0,2,1:T(8,128)(2,1)S(1)}, bf16[512,64,32]{0,2,1:T(8,128)(2,1)}, u32[]{:S(2)}) copy-start(bf16[512,64,32]{0,2,1:T(8,128)(2,1)} %fusion.35) | copy-start | bytes 6291460
  369.4 9.9 %copy-start.4 = (bf16[256,256]{1,0:T(8,128)(2,1)S(1)}, bf16[256,256]{1,0:T(8,128)(2,1)}, u32[]{:S(2)}) copy-start(bf16[256,256]{1,0:T(8,128)(2,1)} %param.23) | copy-start | bytes 393220
Sparse Core Ops, SparseCore 0:
  129.3 157.4 all-reduce.2
where the time goes:
time: 493 us; the launch traced here: 490 us
  local copies, waits for them, and re-layouts  182 us (37%)
  waiting for transfers between devices  158 us (32%)
  matrix products  84 us (17%)
  other arithmetic  52.1 us (11%)
  between operations  13.5 us (3%)
    psum x1, waiting for transfers between devices, on_device(): lax.psum((domain_accumulated.reshape(MESHES * attention_group_amount, -1)...  158 us
    reshape x8, local copies, waits for them, and re-layouts, spread_phase(): tokens.reshape(MESHES, attention_group_amount, partition_amount, head_width)  66.4 us
    dot_general x4, matrix products, partition_routine(): jnp.dot(one_hot.T, partial_sums.reshape(tile_amount, -1))  17.9 us
    sub x4, matrix products, partition_routine(): jax.nn.softmax(partition_scores, axis=-1) * living[:, :, None, None]  14.4 us
    reshape x4, local copies, waits for them, and re-layouts, partition_routine(): partial_sums.reshape(tile_amount, -1)  14 us
    reduce_sum x4, other arithmetic, partition_routine(): partial_totals = jnp.sum(partition_shares.astype(jnp.float32), axis=1)  13.5 us
    dot_general x1, matrix products, attend_tokens(): jnp.einsum('rme,rne->rmn', queries, key_rows) * head_width ** (-0.5)  12.5 us
    gather x4, local copies, waits for them, and re-layouts, spread_phase(): chosen = jnp.take(tables, jnp.minimum(domain_sequence, MESHES - 1), axis=0)  11.7 us
  transfers between devices with their start and end apart: 1, of which 1 were waited for; matrix products, arithmetic and copies ran while one was open for 0% of the time, Pallas kernels for 0%

commit v1 on v0

v1 whole, which is shorter than its diff:
```python
import jax
import jax.numpy as jnp
from jax import lax
from jax.experimental import pallas as pl
from jax.experimental.pallas import tpu as pltpu
from jax.sharding import PartitionSpec as P

MESHES = 64
CHUNK = 4
LOG2E = 1.4426950408889634
AXES = ("grp", "dev")
HIGHEST = lax.Precision.HIGHEST
F32 = jnp.float32
BF16 = jnp.bfloat16


def _dot(a, b, dims, precision=None):
    return lax.dot_general(a, b, (dims, ((), ())), precision=precision, preferred_element_type=F32)


def _living(tal, base, points, block):
    lane = lax.broadcasted_iota(jnp.int32, (1, points), 1)
    limit = jnp.zeros((1, points), jnp.int32)
    for b in range(points // block):
        limit = jnp.where(lane // block == b, b * block + tal[base + b], limit)
    return (lane < limit).astype(F32)


def _last_label(lab, base):
    last = lab[base]
    for b in range(1, CHUNK):
        last = jnp.where(lab[base + b] < MESHES, lab[base + b], last)
    return last


def gather_kernel(
    lab, tal, sharp, x_ref, gain_ref, emb_ref, pin_ref, score_ref,
    w_ref, acc_ref, send_ref, meta_ref,
    wt_ref, st_ref, cs_ref,
):
    step = pl.program_id(0)
    base = step * CHUNK
    _, block, width = x_ref.shape
    points = CHUNK * block
    heads = sharp.shape[0]
    dh = width // heads
    parts = score_ref.shape[1]
    group = heads // 2

    @pl.when(step == 0)
    def _():
        wt_ref[:width, :] = emb_ref[...].astype(F32).T.astype(BF16)
        wt_ref[width:, :] = pin_ref[...].astype(F32).T.astype(BF16)
        st_ref[...] = score_ref[...].astype(F32).T.astype(BF16)
        for h in range(heads):
            cs_ref[h : h + 1, :] = jnp.full((1, points), LOG2E, F32) / jnp.full(
                (1, points), sharp[h], F32
            )
        meta_ref[0] = lab[0]
        meta_ref[1] = lab[0]

        @pl.when(lab[0] >= MESHES)
        def _():
            acc_ref[0] = jnp.zeros(acc_ref.shape[1:], F32)

    @pl.when(lab[base] < MESHES)
    def _():
        x = x_ref[...].reshape(points, width).astype(F32)
        centre = x - jnp.sum(x, axis=1, keepdims=True) * (1.0 / width)
        var = jnp.sum(centre * centre, axis=1, keepdims=True) * (1.0 / width)
        normed = (centre * lax.rsqrt(var + 1e-05) * gain_ref[...]).astype(BF16)
        both = _dot(wt_ref[...], normed, ((1,), (1,))).astype(BF16)
        live = _living(tal, base, points, block)
        for h in range(heads):
            mid = both[width + h * dh : width + (h + 1) * dh, :]
            logit = _dot(st_ref[...], mid, ((1,), (0,)))
            top = jnp.max(logit, axis=0, keepdims=True)
            e = jnp.exp2((logit - top) * cs_ref[h : h + 1, :])
            scale = live / jnp.sum(e, axis=0, keepdims=True)
            w_ref[0, h * parts : (h + 1) * parts, :] = (e * scale).astype(BF16)

        ones = jnp.ones((16, points), BF16)
        low = lab[base]
        high = _last_label(lab, base)
        meta_ref[1] = high
        lane = lax.broadcasted_iota(jnp.int32, (dh, 128), 1)

        def add(mesh, mask):
            slot = mesh - lab[0]
            fresh = jnp.logical_or(step == 0, lab[jnp.maximum(base - 1, 0)] != mesh)
            for g in range(2):
                f = jnp.concatenate([both[g * group * dh : (g + 1) * group * dh, :], ones], axis=0)
                w = w_ref[0, g * group * parts : (g + 1) * group * parts, :]
                if mask is not None:
                    f = jnp.where(mask, f, jnp.zeros_like(f))
                s = _dot(f, w, ((1,), (1,)))
                for t in range(2):
                    tile = s[:, t * 128 : (t + 1) * 128]
                    r = 2 * t * dh
                    own = jnp.where(lane < parts, tile[r : r + dh], tile[r + dh : r + 2 * dh])
                    own = jnp.concatenate([own, tile[group * dh : group * dh + 8]], axis=0)
                    at = (slot, slice(None), slice((2 * g + t) * 128, (2 * g + t + 1) * 128))
                    acc_ref[at] = jnp.where(fresh, own, acc_ref[at] + own)

        @pl.when(low == high)
        def _():
            add(low, None)

        @pl.when(low != high)
        def _():
            where = lax.broadcasted_iota(jnp.int32, (group * dh + 16, points), 1) // block
            which = jnp.full(where.shape, MESHES, jnp.int32)
            for b in range(CHUNK):
                which = jnp.where(where == b, lab[base + b], which)

            @pl.loop(low, high + 1)
            def _(mesh):
                add(mesh, which == mesh)

    @pl.when(step == pl.num_programs(0) - 1)
    def _():
        last = meta_ref[1] - lab[0]
        alone = last == 0
        column = lax.broadcasted_iota(jnp.int32, (128, 128), 1)
        tail = jnp.where(alone, -1, meta_ref[1]).astype(F32)
        send_ref[:, 512:640] = jnp.where(column == 0, lab[0].astype(F32), tail)
        for t in range(4):
            cut = slice(t * 128, (t + 1) * 128)
            row = slice(t * dh, (t + 1) * dh)
            head = acc_ref[0, :, cut]
            foot = acc_ref[last, :, cut]
            foot = jnp.where(alone, jnp.zeros_like(foot), foot)
            send_ref[row, 0:128] = head[:dh]
            send_ref[row, 128:256] = foot[:dh]
            send_ref[row, 256:384] = jnp.broadcast_to(head[dh : dh + 1], (dh, 128))
            send_ref[row, 384:512] = jnp.broadcast_to(foot[dh : dh + 1], (dh, 128))


def owner_kernel(r_ref, o_ref):
    labels = r_ref[:, 512:640]
    first = labels[:, 0:1]
    final = labels[:, 1:2]
    rows = jnp.concatenate([first, final], axis=0)
    rows = jnp.broadcast_to(rows, (256, 256))
    same = (rows == rows.T).astype(F32)
    data = jnp.concatenate(
        [
            jnp.concatenate([r_ref[:, 0:128], r_ref[:, 256:384]], axis=1),
            jnp.concatenate([r_ref[:, 128:256], r_ref[:, 384:512]], axis=1),
        ],
        axis=0,
    )
    whole = _dot(same, data, ((1,), (0,)), HIGHEST)
    tokens = whole[:, :128] / (whole[:, 128:] + 1.0)
    o_ref[:, 0:128] = tokens[:128]
    o_ref[:, 128:256] = tokens[128:]


def spread_kernel(
    lab, tal, meta, x_ref, w_ref, acc_ref, tok_ref, maps_ref, out_proj_ref,
    o_ref,
    mix_ref,
):
    step = pl.program_id(0)
    base = step * CHUNK
    _, block, width = x_ref.shape
    points = CHUNK * block
    dh = maps_ref.shape[1]
    heads = width // dh
    group = heads // 2
    parts = w_ref.shape[1] // heads
    first = meta[0]
    last = meta[1]

    @pl.when(jnp.logical_and(step == 0, first < MESHES))
    def _():
        row = lax.broadcasted_iota(jnp.int32, (128, 128), 0) // parts
        col = lax.broadcasted_iota(jnp.int32, (128, 128), 1) // parts
        paired = row == col
        lane = lax.broadcasted_iota(jnp.int32, (dh, 128), 1)
        mapt = [maps_ref[i].T for i in range(3)]

        @pl.loop(0, last - first + 1)
        def _(slot):
            for t in range(4):
                cut = slice(t * 128, (t + 1) * 128)
                kept = acc_ref[slot, :, cut]
                token = kept[:dh] / (kept[dh : dh + 1] + 1.0)
                token = jnp.where(slot == last - first, tok_ref[t * dh : (t + 1) * dh, 128:256], token)
                token = jnp.where(slot == 0, tok_ref[t * dh : (t + 1) * dh, 0:128], token)
                q, k, v = (_dot(m, token, ((1,), (0,)), HIGHEST) for m in mapt)
                score = _dot(k.T, q, ((1,), (0,)), HIGHEST) * (dh**-0.5 * LOG2E)
                score = jnp.where(paired, score, -1e38)
                e = jnp.exp2(score - jnp.max(score, axis=0, keepdims=True))
                prob = e / jnp.sum(e, axis=0, keepdims=True)
                mixed = _dot(v, prob, ((1,), (0,)), HIGHEST)
                for s in range(2):
                    own = jnp.where(lane // parts == s, mixed, 0.0).astype(BF16)
                    r = ((2 * t + s) % group) * dh
                    c = (t % 2) * 128
                    mix_ref[slot, t // 2, r : r + dh, c : c + 128] = own
                    mix_ref[slot, t // 2, r : r + dh, 128 - c : 256 - c] = jnp.zeros_like(own)

    @pl.when(lab[base] >= MESHES)
    def _():
        o_ref[...] = jnp.zeros(o_ref.shape, BF16)

    @pl.when(lab[base] < MESHES)
    def _():
        low = lab[base]
        high = _last_label(lab, base)
        rows = group * parts

        def finish(spread, x, live):
            projected = _dot(spread, out_proj_ref[...], ((0,), (0,)))
            return ((x.astype(F32) + projected) * live).astype(BF16)

        def alive(limit, count):
            point = lax.broadcasted_iota(jnp.int32, (count, width), 0)
            return point < limit

        @pl.when(low == high)
        def _():
            slot = low - first
            spread = jnp.concatenate(
                [
                    _dot(mix_ref[slot, g], w_ref[0, g * rows : (g + 1) * rows, :], ((1,), (0,)))
                    for g in range(2)
                ],
                axis=0,
            ).astype(BF16)
            projected = _dot(spread, out_proj_ref[...], ((0,), (0,)))
            for b in range(CHUNK):
                whole = x_ref[b].astype(F32) + projected[b * block : (b + 1) * block]
                o_ref[b] = jnp.where(alive(tal[base + b], block), whole, 0.0).astype(BF16)

        @pl.when(low != high)
        def _():
            for b in range(CHUNK):
                slot = jnp.minimum(lab[base + b], high) - first
                cut = slice(b * block, (b + 1) * block)
                spread = jnp.concatenate(
                    [
                        _dot(mix_ref[slot, g], w_ref[0, g * rows : (g + 1) * rows, cut], ((1,), (0,)))
                        for g in range(2)
                    ],
                    axis=0,
                ).astype(BF16)
                projected = _dot(spread, out_proj_ref[...], ((0,), (0,)))
                whole = x_ref[b].astype(F32) + projected
                o_ref[b] = jnp.where(alive(tal[base + b], block), whole, 0.0).astype(BF16)


def on_device(
    vertex_values,
    position_domain_label,
    position_vertex_tally,
    normalizer_gain,
    embedding_matrix,
    partition_input_matrix,
    partition_score_matrix,
    softmax_sharpness,
    partition_attention_maps,
    readout_matrix,
):
    slots, block, width = vertex_values.shape
    heads = softmax_sharpness.shape[0]
    dh, parts = partition_score_matrix.shape
    steps = slots // CHUNK
    points = CHUNK * block
    local = slots // 2 + 1
    local = local + 1
    whole = lambda *shape: pl.BlockSpec(shape, lambda i, *_: (0,) * len(shape))
    chunk = pl.BlockSpec((CHUNK, block, width), lambda i, *_: (i, 0, 0))
    weight = pl.BlockSpec((1, heads * parts, points), lambda i, *_: (i, 0, 0))
    shares, sums, send, meta = pl.pallas_call(
        gather_kernel,
        name="gather",
        grid_spec=pltpu.PrefetchScalarGridSpec(
            num_scalar_prefetch=3,
            grid=(steps,),
            in_specs=[
                chunk,
                whole(1, width),
                whole(width, width),
                whole(width, width),
                whole(dh, parts),
            ],
            out_specs=[
                weight,
                whole(local, dh + 8, heads * parts),
                whole(128, 640),
                pl.BlockSpec(memory_space=pltpu.SMEM),
            ],
            scratch_shapes=[
                pltpu.VMEM((2 * width, width), BF16),
                pltpu.VMEM((parts, dh), BF16),
                pltpu.VMEM((heads, points), F32),
            ],
        ),
        out_shape=[
            jax.ShapeDtypeStruct((steps, heads * parts, points), BF16),
            jax.ShapeDtypeStruct((local, dh + 8, heads * parts), F32),
            jax.ShapeDtypeStruct((128, 640), F32),
            jax.ShapeDtypeStruct((8,), jnp.int32),
        ],
        compiler_params=pltpu.CompilerParams(dimension_semantics=("arbitrary",)),
    )(
        position_domain_label,
        position_vertex_tally,
        softmax_sharpness,
        vertex_values,
        normalizer_gain.reshape(1, width),
        embedding_matrix,
        partition_input_matrix,
        partition_score_matrix,
    )
    got = lax.all_to_all(send, AXES, 0, 0, tiled=True)
    back = pl.pallas_call(
        owner_kernel, name="owner", out_shape=jax.ShapeDtypeStruct((128, 256), F32)
    )(got)
    tokens = lax.all_to_all(back, AXES, 0, 0, tiled=True)
    return pl.pallas_call(
        spread_kernel,
        name="spread",
        grid_spec=pltpu.PrefetchScalarGridSpec(
            num_scalar_prefetch=3,
            grid=(steps,),
            in_specs=[
                chunk,
                weight,
                whole(local, dh + 8, heads * parts),
                whole(128, 256),
                whole(3, dh, dh),
                whole(width, width),
            ],
            out_specs=chunk,
            scratch_shapes=[pltpu.VMEM((local, 2, width // 2, heads * parts // 2), BF16)],
        ),
        out_shape=jax.ShapeDtypeStruct(vertex_values.shape, BF16),
        compiler_params=pltpu.CompilerParams(dimension_semantics=("arbitrary",)),
    )(
        position_domain_label,
        position_vertex_tally,
        meta,
        vertex_values,
        shares,
        sums,
        tokens,
        partition_attention_maps,
        readout_matrix,
    )


def solution(mesh):
    rows = P(AXES)
    return jax.shard_map(
        on_device,
        mesh=mesh,
        in_specs=(P(AXES, None, None), rows, rows, P(), P(), P(), P(), P(), P(), P()),
        out_specs=P(AXES, None, None),
        check_vma=False,
    )
```

time: 493 us -> 101 us (0.20)
  local copies, waits for them, and re-layouts: 182 us -> 3.76 us
  waiting for transfers between devices: 158 us -> 0 us
  matrix products: 84 us -> 0 us
  Pallas kernels: 0 us -> 59.9 us
  other arithmetic: 52.1 us -> 0 us
  blocking collectives: 0 us -> 35.9 us
  between operations: 13.5 us -> 0.02 us
    psum x1 -> x0, waiting for transfers between devices: 158 us -> none  [on_device(): lax.psum((domain_accumulated.reshape(MESHES * attention_group_amount, -1)...]
    reshape x21 -> x0, local copies, waits for them, and re-layouts: 88.1 us -> none  [the longest x8 66.4 us: spread_phase(): tokens.reshape(MESHES, attention_group_amount, partition_amount, head_width)]
    dot_general x33 -> x0, matrix products: 69.7 us -> none  [the longest x4 17.9 us: partition_routine(): jnp.dot(one_hot.T, partial_sums.reshape(tile_amount, -1))]
    pallas_call x0 -> x3, Pallas kernels: none -> 59.9 us  [the longest x1 31.8 us: on_device(): pl.pallas_call(spread_kernel, name='spread', grid_spec=pltpu.PrefetchScal...]
    reduce_sum x13 -> x0, other arithmetic: 37.7 us -> none  [the longest x4 13.5 us: partition_routine(): partial_totals = jnp.sum(partition_shares.astype(jnp.float32), axis=1)]
    all_to_all x0 -> x2, blocking collectives: none -> 35.9 us  [the longest x1 21.9 us: on_device(): got = lax.all_to_all(send, AXES, 0, 0, tiled=True)]
    dot_general x3 -> x0, local copies, waits for them, and re-layouts: 25.6 us -> none  [the longest x1 8.94 us: attend_tokens(): key_rows = jnp.einsum('rmd,de->rme', tokens, partition_attention_maps[1])]
    convert_element_type x13 -> x0, local copies, waits for them, and re-layouts: 18.2 us -> none  [the longest x1 6.93 us: attend_tokens(): blended.reshape(row_count, partition_amount * head_width)]
  transfers between devices with their start and end apart: 1 -> 0, of which waited for: 1 -> 0; matrix products, arithmetic and copies ran while one was open for 0% -> 0% of each run, Pallas kernels for 0% -> 0%
where the time goes in v1:
time: 101 us; the launch traced here: 99.6 us
  Pallas kernels  59.9 us (59%)
  blocking collectives  35.9 us (36%)
  local copies, waits for them, and re-layouts  3.76 us (4%)
    pallas_call x1, Pallas kernels, on_device(): pl.pallas_call(spread_kernel, name='spread', grid_spec=pltpu.PrefetchScal...  31.8 us
    pallas_call x1, Pallas kernels, on_device(): pl.pallas_call(gather_kernel, name='gather', grid_spec=pltpu.PrefetchScal...  25.9 us
    all_to_all x1, blocking collectives, on_device(): got = lax.all_to_all(send, AXES, 0, 0, tiled=True)  21.9 us
    all_to_all x1, blocking collectives, on_device(): tokens = lax.all_to_all(back, AXES, 0, 0, tiled=True)  14 us
    pallas_call x1, Pallas kernels, on_device(): pl.pallas_call(owner_kernel, name='owner', out_shape=jax.ShapeDtypeStruct...  2.18 us

profile of v1, /device:TPU:1, one launch (start us, length us, event | category | flops | bytes accessed | tf_op | source)
XLA Modules:
  0.0 99.6 jit_solution(12497723972688453730)
XLA Ops:
  0.0 25.9 %gather.1 = (bf16[16,512,512]{2,1,0:T(8,128)(2,1)}, f32[34,40,512]{2,1,0:T(8,128)}, f32[128,640]{1,0:T(8,128)}, s32[8]{0:T(128)}) custom-call(s32[64]{0:T(128)} %lab.3, s32[64]{0:T(128)} %tal.3, f32[8]{0:T(128)} %sharp.1, bf16[64,128,256]{2,1,0:T(8,128)(2,1)} %x_ref.3, f32[1,256]{1,0:T(1,128)} %bitcast.13, bf16[256,256]{1,0:T(8,128)(2,1)} %emb_ref.1, ...), custom_call_target="tpu_custom_call" | custom-call | tf_op jit(solution)/shard_map/gather/pallas_call | solution.py:276
  25.9 1.3 %copy.11 = f32[128,1,640]{2,1,0:T(1,128)S(1)} copy(f32[128,1,640]{2,0,1:T(8,128)} %bitcast.12) | data formatting | bytes 655360 | tf_op jit(solution)/shard_map/all_to_all | solution.py:318
  27.3 21.9 %all_to_all.22 = f32[128,1,640]{2,1,0:T(1,128)S(1)} all-to-all(f32[128,1,640]{2,1,0:T(1,128)S(1)} %copy.11), channel_id=1, replica_groups=mesh['grp'=8,'dev'=16] {'grp','dev'}, dimensions={0} | all-to-all | bytes 655360 | tf_op jit(solution)/shard_map/all_to_all | solution.py:318
  49.2 0.7 copy.17
  49.9 2.2 %owner.1 = f32[128,256]{1,0:T(8,128)} custom-call(f32[128,640]{1,0:T(8,128)} %bitcast.9), custom_call_target="tpu_custom_call" | custom-call | tf_op jit(solution)/shard_map/owner/pallas_call | solution.py:319
  52.1 1.0 %copy.12 = f32[128,1,256]{2,1,0:T(1,128)S(1)} copy(f32[128,1,256]{2,0,1:T(8,128)} %bitcast.11) | data formatting | bytes 262144 | tf_op jit(solution)/shard_map/all_to_all | solution.py:322
  53.1 14.0 %all_to_all.23 = f32[128,1,256]{2,1,0:T(1,128)S(1)} all-to-all(f32[128,1,256]{2,1,0:T(1,128)S(1)} %copy.12), channel_id=1, replica_groups=mesh['grp'=8,'dev'=16] {'grp','dev'}, dimensions={0} | all-to-all | bytes 262144 | tf_op jit(solution)/shard_map/all_to_all | solution.py:322
  67.1 0.7 copy.18
  67.8 31.8 %spread.1 = bf16[64,128,256]{2,1,0:T(8,128)(2,1)} custom-call(s32[64]{0:T(128)} %lab.3, s32[64]{0:T(128)} %tal.3, s32[8]{0:T(128)} %get-tuple-element.9.meta, bf16[64,128,256]{2,1,0:T(8,128)(2,1)} %x_ref.3, bf16[16,512,512]{2,1,0:T(8,128)(2,1)} %get-tuple-element.10.w_ref, f32[34,40,512]{2,1,0:T(8,128)} %get-tuple-element.11.acc_ref, f32[128,256]{1,0:T(8,128)} %bitcast.10, ...), custom_call_target="tpu_custom_call" | custom-call | tf_op jit(solution)/shard_map/spread/pallas_call | solution.py:323

commit v2 on v0

v2 whole, which is shorter than its diff:
```python
import jax
import jax.numpy as jnp
from jax import lax
from jax.experimental import pallas as pl
from jax.experimental.pallas import tpu as pltpu
from jax.sharding import PartitionSpec as P

MESHES = 64
UNIT = 4
PIECE = 4
BATCH = 4
LOG2E = 1.4426950408889634
AXES = ("grp", "dev")
F32 = jnp.float32
BF16 = jnp.bfloat16
HIGHEST = lax.Precision.HIGHEST


def _dot(a, b, dims, precision=None):
    return lax.dot_general(a, b, (dims, ((), ())), precision=precision, preferred_element_type=F32)


def _split(a, terms):
    out = []
    for _ in range(terms):
        out.append(a.astype(BF16))
        a = a - out[-1].astype(F32)
    return out


def _dot3(a, b):
    ah, al = _split(a, 2)
    bh, bl = _split(b, 2)
    return _dot(
        jnp.concatenate([ah, al, ah], axis=1), jnp.concatenate([bh, bh, bl], axis=0), ((1,), (0,))
    )


def _units(lab, start, slot, blocks):
    def visit(b, carry):
        count, begin = carry
        mesh = lab[b]
        before = lab[jnp.maximum(b - 1, 0)]
        opens = jnp.logical_or(jnp.logical_or(b == 0, mesh != before), b - begin == UNIT)
        opens = jnp.logical_and(opens, mesh < MESHES)

        @pl.when(opens)
        def _():
            start[count] = b
            slot[count] = mesh - lab[0]

        return count + opens.astype(jnp.int32), jnp.where(opens, b, begin)

    used = jnp.int32(0)
    for b in range(blocks):
        used = used + (lab[b] < MESHES).astype(jnp.int32)
    count, _ = lax.fori_loop(0, blocks, visit, (jnp.int32(0), jnp.int32(0)))
    return count, used


def gather_kernel(
    lab, tal, sharp, x_hbm, gain_hbm, emb_hbm, pin_hbm, score_hbm,
    x_ref, w_ref, acc_ref, send_ref, start, slot, meta,
    gain_ref, emb_ref, pin_ref, score_ref, wt_ref, st_ref, mean_ref, f_ref, sems, param_sems,
):
    blocks, block, width = x_hbm.shape
    points = UNIT * block
    heads = sharp.shape[0]
    dh = width // heads
    parts = score_ref.shape[1]
    group = heads // 2
    spare = acc_ref.shape[0] - 1
    pieces = blocks // PIECE

    def copy(i):
        part = pl.ds(i * PIECE, PIECE)
        return pltpu.make_async_copy(x_hbm.at[part], x_ref.at[part], sems.at[i])

    given = ((gain_hbm, gain_ref), (emb_hbm, emb_ref), (pin_hbm, pin_ref), (score_hbm, score_ref))
    params = [pltpu.make_async_copy(a, b, param_sems.at[n]) for n, (a, b) in enumerate(given)]
    for p in params:
        p.start()
    for i in range(pieces):
        copy(i).start()
    row = lax.broadcasted_iota(jnp.int32, (width, width), 0)
    col = lax.broadcasted_iota(jnp.int32, (width, width), 1)
    mean_ref[...] = ((row == col).astype(F32) - 1.0 / width).astype(BF16)
    count, used = _units(lab, start, slot, blocks)
    start[count] = used
    for n in range(BATCH):
        start[count + 1 + n] = blocks
        slot[count + n] = spare
    meta[0] = lab[0]
    meta[1] = count
    meta[2] = used
    last = jnp.where(used > 0, slot[jnp.maximum(count - 1, 0)], 0)
    meta[3] = last
    for p in params:
        p.wait()
    gain_ref[...] = gain_ref[...] * width**0.5
    wt_ref[:width, :] = emb_ref[...].astype(F32).T.astype(BF16)
    wt_ref[width:, :] = pin_ref[...].astype(F32).T.astype(BF16)
    score = score_ref[...].astype(F32).T
    for h in range(heads):
        factor = jnp.full(score.shape, LOG2E, F32) / jnp.full(score.shape, sharp[h], F32)
        st_ref[h] = jnp.concatenate(_split(score * factor, 3), axis=1)

    group_points = group * dh
    ones = jnp.ones((16, block), BF16)
    lane = lax.broadcasted_iota(jnp.int32, (dh, 128), 1)

    def normalize(s):
        x = x_ref[pl.ds(s, UNIT)].reshape(points, width)
        centre = _dot(x, mean_ref[...], ((1,), (0,)))
        return centre

    def scale(centre):
        square = jnp.sum(centre * centre, axis=1, keepdims=True)
        return (centre * lax.rsqrt(square + 1e-05 * width) * gain_ref[...]).astype(BF16)

    def weigh(logit, live):
        e = jnp.exp2(logit - jnp.max(logit, axis=0, keepdims=True))
        return (e * (live / jnp.sum(e, axis=0, keepdims=True))).astype(BF16)

    def living(s):
        spot = lax.broadcasted_iota(jnp.int32, (1, points), 1)
        limit = jnp.zeros((1, points), jnp.int32)
        for b in range(UNIT):
            limit = jnp.where(spot // block == b, b * block + tal[s + b], limit)
        return (spot < limit).astype(F32)

    def put(ref, s, row, value):
        for b in range(UNIT):
            ref[s + b, row : row + value.shape[0], :] = value[:, b * block : (b + 1) * block]

    for i in range(pieces):
        copy(i).wait()

    trips = (used + BATCH * UNIT - 1) // (BATCH * UNIT)

    @pl.loop(0, trips)
    def _(j):
        first = [(j * BATCH + n) * UNIT for n in range(BATCH)]
        centres = [normalize(s) for s in first]
        normed = [scale(c) for c in centres]
        both = [_dot(wt_ref[...], n, ((1,), (1,))).astype(BF16) for n in normed]
        for s, a in zip(first, both):
            put(f_ref, s, 0, a[:width])
        lives = [living(s) for s in first]
        items = [(h, n) for h in range(heads) for n in range(BATCH)]
        ahead = {}
        for at in range(len(items) + BATCH):
            if at < len(items):
                h, n = items[at]
                mid = both[n][width + h * dh : width + (h + 1) * dh, :]
                ahead[h, n] = _dot(st_ref[h], jnp.concatenate([mid, mid, mid], axis=0), ((1,), (0,)))
            if at >= BATCH:
                h, n = items[at - BATCH]
                put(w_ref, first[n], h * parts, weigh(ahead.pop((h, n)), lives[n]))

    for b in range(UNIT):
        w_ref[trips * BATCH * UNIT + b] = jnp.zeros(w_ref.shape[1:], BF16)

    def product(n, g):
        s = start[n]
        f = []
        for b in range(UNIT):
            part = jnp.concatenate([f_ref[s + b, g * group_points : (g + 1) * group_points], ones], axis=0)
            f.append(jnp.where(s + b < start[n + 1], part, jnp.zeros_like(part)))
        rows = slice(g * group * parts, (g + 1) * group * parts)
        w = jnp.concatenate([w_ref[s + b, rows] for b in range(UNIT)], axis=1)
        return _dot(jnp.concatenate(f, axis=1), w, ((1,), (1,)))

    @pl.loop(0, (count + BATCH - 1) // BATCH)
    def _(j):
        units = [j * BATCH + n for n in range(BATCH)]
        totals = [(n, g, product(n, g)) for n in units for g in range(2)]
        for n, g, total in totals:
            here = slot[n]
            fresh = jnp.logical_or(n == 0, slot[jnp.maximum(n - 1, 0)] != here)
            for t in range(2):
                tile = total[:, t * 128 : (t + 1) * 128]
                r = 2 * t * dh
                own = jnp.where(lane < parts, tile[r : r + dh], tile[r + dh : r + 2 * dh])
                own = jnp.concatenate([own, tile[group_points : group_points + 8]], axis=0)
                at = (here, slice(None), slice((2 * g + t) * 128, (2 * g + t + 1) * 128))
                acc_ref[at] = jnp.where(fresh, own, acc_ref[at] + own)

    @pl.when(used == 0)
    def _():
        acc_ref[0] = jnp.zeros(acc_ref.shape[1:], F32)

    alone = last == 0
    column = lax.broadcasted_iota(jnp.int32, (128, 128), 1)
    tail = jnp.where(alone, -1, lab[0] + last).astype(F32)
    send_ref[:, 512:640] = jnp.where(column == 0, lab[0].astype(F32), tail)
    for t in range(4):
        cut = slice(t * 128, (t + 1) * 128)
        at = slice(t * dh, (t + 1) * dh)
        head = acc_ref[0, :, cut]
        foot = acc_ref[last, :, cut]
        foot = jnp.where(alone, jnp.zeros_like(foot), foot)
        send_ref[at, 0:128] = head[:dh]
        send_ref[at, 128:256] = foot[:dh]
        send_ref[at, 256:384] = jnp.broadcast_to(head[dh : dh + 1], (dh, 128))
        send_ref[at, 384:512] = jnp.broadcast_to(foot[dh : dh + 1], (dh, 128))


def owner_kernel(r_ref, o_ref):
    labels = r_ref[:, 512:640]
    rows = jnp.concatenate([labels[:, 0:1], labels[:, 1:2]], axis=0)
    rows = jnp.broadcast_to(rows, (256, 256))
    same = (rows == rows.T).astype(F32)
    data = jnp.concatenate(
        [
            jnp.concatenate([r_ref[:, 0:128], r_ref[:, 256:384]], axis=1),
            jnp.concatenate([r_ref[:, 128:256], r_ref[:, 384:512]], axis=1),
        ],
        axis=0,
    )
    whole = _dot(same, data, ((1,), (0,)), HIGHEST)
    tokens = whole[:, :128] / (whole[:, 128:] + 1.0)
    o_ref[:, 0:128] = tokens[:128]
    o_ref[:, 128:256] = tokens[128:]


def spread_kernel(
    tal, start, slot, meta, x_ref, w_ref, acc_ref, tok_ref, maps_ref, out_proj_ref,
    o_hbm,
    o_ref, mix_ref, sems,
):
    blocks, block, width = o_hbm.shape
    dh = maps_ref.shape[1]
    heads = width // dh
    group = heads // 2
    parts = w_ref.shape[1] // heads
    rows = group * parts
    count = meta[1]
    used = meta[2]
    last = meta[3]
    pieces = blocks // PIECE
    spare = mix_ref.shape[0] - 1

    def copy(i):
        part = pl.ds(i * PIECE, PIECE)
        return pltpu.make_async_copy(o_ref.at[part], o_hbm.at[part], sems.at[i])

    def attend(ats):
        row = lax.broadcasted_iota(jnp.int32, (128, 128), 0) // parts
        col = lax.broadcasted_iota(jnp.int32, (128, 128), 1) // parts
        lane = lax.broadcasted_iota(jnp.int32, (dh, 128), 1)
        maps = jnp.concatenate([maps_ref[i].T for i in range(3)], axis=0)
        projected = []
        for at in ats:
            tokens = []
            for t in range(4):
                kept = acc_ref[at, :, t * 128 : (t + 1) * 128]
                token = kept[:dh] / (kept[dh : dh + 1] + 1.0)
                token = jnp.where(at == last, tok_ref[t * dh : (t + 1) * dh, 128:256], token)
                tokens.append(jnp.where(at == 0, tok_ref[t * dh : (t + 1) * dh, 0:128], token))
            projected.append(_dot3(maps, jnp.concatenate(tokens, axis=1)))
        tiles = [(n, t) for n in range(len(ats)) for t in range(4)]
        scores = []
        for n, t in tiles:
            q, k = (projected[n][i * dh : (i + 1) * dh, t * 128 : (t + 1) * 128] for i in range(2))
            kh, kl = _split(k * (dh**-0.5 * LOG2E), 2)
            qh, ql = _split(q, 2)
            left = jnp.concatenate([kh, kl, kh], axis=0)
            scores.append(_dot(left, jnp.concatenate([qh, qh, ql], axis=0), ((0,), (0,))))
        probs = []
        for score in scores:
            score = jnp.where(row == col, score, -1e38)
            e = jnp.exp2(score - jnp.max(score, axis=0, keepdims=True))
            probs.append(e / jnp.sum(e, axis=0, keepdims=True))
        mixes = [
            _dot3(projected[n][2 * dh :, t * 128 : (t + 1) * 128], prob)
            for (n, t), prob in zip(tiles, probs)
        ]
        for (n, t), mixed in zip(tiles, mixes):
            for s in range(2):
                own = jnp.where(lane // parts == s, mixed, 0.0).astype(BF16)
                r = ((2 * t + s) % group) * dh
                c = (t % 2) * 128
                mix_ref[ats[n], t // 2, r : r + dh, c : c + 128] = own
                mix_ref[ats[n], t // 2, r : r + dh, 128 - c : 256 - c] = jnp.zeros_like(own)

    def blend(n):
        s = start[n]
        return jnp.concatenate(
            [
                _dot(
                    mix_ref[slot[n], g],
                    jnp.concatenate([w_ref[s + b, g * rows : (g + 1) * rows] for b in range(UNIT)], axis=1),
                    ((1,), (0,)),
                )
                for g in range(2)
            ],
            axis=0,
        ).astype(BF16)

    def finish(n, mixed):
        s = start[n]
        point = lax.broadcasted_iota(jnp.int32, (block, width), 0)
        projected = _dot(mixed, out_proj_ref[...], ((0,), (0,)))
        for b in range(UNIT):
            whole = x_ref[s + b].astype(F32) + projected[b * block : (b + 1) * block]
            live = point < tal[jnp.minimum(s + b, blocks - 1)]
            o_ref[s + b] = jnp.where(live, whole, 0.0).astype(BF16)

    @pl.loop(used // PIECE * PIECE, blocks)
    def _(b):
        o_ref[b] = jnp.zeros((block, width), BF16)

    idle = (used + PIECE - 1) // PIECE

    @pl.when(used > 0)
    def _():
        @pl.loop(0, (last + 2) // 2)
        def _(j):
            attend([2 * j, jnp.where(2 * j + 1 > last, spare, 2 * j + 1)])

    def step(j, sent):
        units = [BATCH * j + n for n in range(BATCH)]
        mixed = [blend(n) for n in units]
        for n, m in zip(units, mixed):
            finish(n, m)
        final = start[jnp.minimum(BATCH * (j + 1), count)]
        final = jnp.where(final == used, idle, final // PIECE)

        @pl.loop(sent, final)
        def _(i):
            copy(i).start()

        return final

    lax.fori_loop(0, (count + BATCH - 1) // BATCH, step, jnp.int32(0))

    @pl.loop(idle, pieces)
    def _(i):
        copy(i).start()

    for i in range(pieces):
        copy(i).wait()


def on_device(
    vertex_values,
    position_domain_label,
    position_vertex_tally,
    normalizer_gain,
    embedding_matrix,
    partition_input_matrix,
    partition_score_matrix,
    softmax_sharpness,
    partition_attention_maps,
    readout_matrix,
):
    slots, block, width = vertex_values.shape
    heads = softmax_sharpness.shape[0]
    dh, parts = partition_score_matrix.shape
    points = UNIT * block
    pieces = slots // PIECE
    room = slots + UNIT
    local = slots // 2 + 2
    smem = pl.BlockSpec(memory_space=pltpu.SMEM)
    vmem = pl.BlockSpec(memory_space=pltpu.VMEM)
    hbm = pl.BlockSpec(memory_space=pltpu.HBM)
    params = pltpu.CompilerParams(vmem_limit_bytes=24 << 20)
    far = lambda a: pltpu.with_memory_space_constraint(a, pltpu.HBM)
    x, shares, sums, send, start, slot, meta = pl.pallas_call(
        gather_kernel,
        name="gather",
        in_specs=[smem, smem, smem, hbm, hbm, hbm, hbm, hbm],
        out_specs=[vmem, vmem, vmem, vmem, smem, smem, smem],
        out_shape=[
            pltpu.VMEM((room, block, width), BF16),
            pltpu.VMEM((room, heads * parts, block), BF16),
            pltpu.VMEM((local, dh + 8, heads * parts), F32),
            jax.ShapeDtypeStruct((128, 640), F32),
            jax.ShapeDtypeStruct((2 * slots,), jnp.int32),
            jax.ShapeDtypeStruct((2 * slots,), jnp.int32),
            jax.ShapeDtypeStruct((8,), jnp.int32),
        ],
        scratch_shapes=[
            pltpu.VMEM((1, width), F32),
            pltpu.VMEM((width, width), BF16),
            pltpu.VMEM((width, width), BF16),
            pltpu.VMEM((dh, parts), BF16),
            pltpu.VMEM((2 * width, width), BF16),
            pltpu.VMEM((heads, parts, 3 * dh), BF16),
            pltpu.VMEM((width, width), BF16),
            pltpu.VMEM((room, width, block), BF16),
            pltpu.SemaphoreType.DMA((pieces,)),
            pltpu.SemaphoreType.DMA((4,)),
        ],
        compiler_params=params,
    )(
        far(position_domain_label),
        far(position_vertex_tally),
        far(softmax_sharpness),
        far(vertex_values),
        far(normalizer_gain.reshape(1, width)),
        far(embedding_matrix),
        far(partition_input_matrix),
        far(partition_score_matrix),
    )
    got = lax.all_to_all(send, AXES, 0, 0, tiled=True)
    back = pl.pallas_call(
        owner_kernel,
        name="owner",
        out_shape=jax.ShapeDtypeStruct((128, 256), F32),
        compiler_params=params,
    )(got)
    tokens = lax.all_to_all(back, AXES, 0, 0, tiled=True)
    keep = lambda a: pltpu.with_memory_space_constraint(a, pltpu.VMEM)
    return pl.pallas_call(
        spread_kernel,
        name="spread",
        in_specs=[smem, smem, smem, smem, vmem, vmem, vmem, vmem, vmem, vmem],
        out_specs=hbm,
        out_shape=jax.ShapeDtypeStruct(vertex_values.shape, BF16),
        scratch_shapes=[
            pltpu.VMEM((room, block, width), BF16),
            pltpu.VMEM((local, 2, width // 2, heads * parts // 2), BF16),
            pltpu.SemaphoreType.DMA((pieces,)),
        ],
        compiler_params=params,
    )(
        position_vertex_tally,
        start,
        slot,
        meta,
        keep(x),
        keep(shares),
        keep(sums),
        tokens,
        partition_attention_maps,
        readout_matrix,
    )


def solution(mesh):
    rows = P(AXES)
    return jax.shard_map(
        on_device,
        mesh=mesh,
        in_specs=(P(AXES, None, None), rows, rows, P(), P(), P(), P(), P(), P(), P()),
        out_specs=P(AXES, None, None),
        check_vma=False,
    )
```

time: 493 us -> 62.6 us (0.13)
  local copies, waits for them, and re-layouts: 182 us -> 0.52 us
  waiting for transfers between devices: 158 us -> 0 us
  matrix products: 84 us -> 0 us
  other arithmetic: 52.1 us -> 0 us
  blocking collectives: 0 us -> 37.5 us
  Pallas kernels: 0 us -> 23.6 us
  between operations: 13.5 us -> 0.07 us
    psum x1 -> x0, waiting for transfers between devices: 158 us -> none  [on_device(): lax.psum((domain_accumulated.reshape(MESHES * attention_group_amount, -1)...]
    reshape x21 -> x0, local copies, waits for them, and re-layouts: 88.1 us -> none  [the longest x8 66.4 us: spread_phase(): tokens.reshape(MESHES, attention_group_amount, partition_amount, head_width)]
    dot_general x33 -> x0, matrix products: 69.7 us -> none  [the longest x4 17.9 us: partition_routine(): jnp.dot(one_hot.T, partial_sums.reshape(tile_amount, -1))]
    reduce_sum x13 -> x0, other arithmetic: 37.7 us -> none  [the longest x4 13.5 us: partition_routine(): partial_totals = jnp.sum(partition_shares.astype(jnp.float32), axis=1)]
    all_to_all x0 -> x2, blocking collectives: none -> 37.5 us  [the longest x1 23.5 us: on_device(): got = lax.all_to_all(send, AXES, 0, 0, tiled=True)]
    dot_general x3 -> x0, local copies, waits for them, and re-layouts: 25.6 us -> none  [the longest x1 8.94 us: attend_tokens(): key_rows = jnp.einsum('rmd,de->rme', tokens, partition_attention_maps[1])]
    pallas_call x0 -> x3, Pallas kernels: none -> 23.6 us  [the longest x1 17 us: on_device(): pl.pallas_call(gather_kernel, name='gather', in_specs=[smem, smem, smem,...]
    convert_element_type x13 -> x0, local copies, waits for them, and re-layouts: 18.2 us -> none  [the longest x1 6.93 us: attend_tokens(): blended.reshape(row_count, partition_amount * head_width)]
  transfers between devices with their start and end apart: 1 -> 0, of which waited for: 1 -> 0; matrix products, arithmetic and copies ran while one was open for 0% -> 0% of each run, Pallas kernels for 0% -> 0%
where the time goes in v2:
time: 62.6 us; the launch traced here: 61.7 us
  blocking collectives  37.5 us (60%)
  Pallas kernels  23.6 us (38%)
    all_to_all x1, blocking collectives, on_device(): got = lax.all_to_all(send, AXES, 0, 0, tiled=True)  23.5 us
    pallas_call x1, Pallas kernels, on_device(): pl.pallas_call(gather_kernel, name='gather', in_specs=[smem, smem, smem,...  17 us
    all_to_all x1, blocking collectives, on_device(): tokens = lax.all_to_all(back, AXES, 0, 0, tiled=True)  14 us
    pallas_call x1, Pallas kernels, on_device(): pl.pallas_call(spread_kernel, name='spread', in_specs=[smem, smem, smem,...  6.08 us

profile of v2, /device:TPU:1, one launch (start us, length us, event | category | flops | bytes accessed | tf_op | source)
XLA Modules:
  0.0 61.7 jit_solution(8598281572224529790)
XLA Ops:
  0.0 0.0 copy-start.2
  0.0 0.0 copy-start
  0.0 0.0 copy-start.1
  0.0 17.0 %gather.1 = (bf16[68,128,256]{2,1,0:T(8,128)(2,1)S(1)}, bf16[68,512,128]{2,1,0:T(8,128)(2,1)S(1)}, f32[34,40,512]{2,1,0:T(8,128)S(1)}, f32[128,640]{1,0:T(8,128)...) custom-call(s32[64]{0:T(128)} %lab.1, s32[64]{0:T(128)} %tal.3, f32[8]{0:T(128)} %sharp.1, ...), custom_call_target="tpu_custom_call" | custom-call | tf_op jit(solution)/shard_map/gather/pallas_call | solution.py:370
  17.0 0.3 copy.11
  17.3 23.5 %all_to_all.22 = f32[128,1,640]{2,1,0:T(1,128)S(1)} all-to-all(f32[128,1,640]{2,1,0:T(1,128)S(1)} %copy.11), channel_id=1, replica_groups=mesh['grp'=8,'dev'=16] {'grp','dev'}, dimensions={0} | all-to-all | bytes 655360 | tf_op jit(solution)/shard_map/all_to_all | solution.py:407
  40.8 0.6 owner.1
  41.4 0.1 copy.12
  41.5 14.0 %all_to_all.23 = f32[128,1,256]{2,1,0:T(1,128)S(1)} all-to-all(f32[128,1,256]{2,1,0:T(1,128)S(1)} %copy.12), channel_id=1, replica_groups=mesh['grp'=8,'dev'=16] {'grp','dev'}, dimensions={0} | all-to-all | bytes 262144 | tf_op jit(solution)/shard_map/all_to_all | solution.py:414
  55.5 0.0 copy-done.2
  55.6 0.0 copy-done
  55.6 0.0 copy-done.1
  55.6 6.1 %spread.1 = bf16[64,128,256]{2,1,0:T(8,128)(2,1)} custom-call(s32[64]{0:T(128)S(1)} %copy-done.2, s32[128]{0:T(128)S(1)} %get-tuple-element.12.start, s32[128]{0:T(128)S(1)} %get-tuple-element.13.slot, s32[8]{0:T(128)S(1)} %get-tuple-element.14.meta, bf16[68,128,256]{2,1,0:T(8,128)(2,1)S(1)} %get-tuple-element.15.x_ref, ...), custom_call_target="tpu_custom_call" | custom-call | tf_op jit(solution)/shard_map/spread/pallas_call | solution.py:416
  (2 shorter events, 0.0 us)
Async XLA Ops:
  0.0 55.6 %copy-start.2 = (s32[64]{0:T(128)S(1)}, s32[64]{0:T(128)}, u32[]{:S(2)}) copy-start(s32[64]{0:T(128)} %tal.3) | copy-start | bytes 772
  0.0 55.6 %copy-start = (bf16[256,256]{1,0:T(8,128)(2,1)S(1)}, bf16[256,256]{1,0:T(8,128)(2,1)}, u32[]{:S(2)}) copy-start(bf16[256,256]{1,0:T(8,128)(2,1)} %out_proj_ref.1) | copy-start | bytes 393220
  0.0 55.6 %copy-start.1 = (f32[3,32,32]{2,1,0:T(8,128)S(1)}, f32[3,32,32]{2,1,0:T(8,128)}, u32[]{:S(2)}) copy-start(f32[3,32,32]{2,1,0:T(8,128)} %maps_ref.1) | copy-start | bytes 36868

commit v3 on v2

--- a/solution.py
+++ b/solution.py
@@ -9,6 +9,7 @@
 UNIT = 4
 PIECE = 4
 BATCH = 4
+WIDE = 8
 LOG2E = 1.4426950408889634
 AXES = ("grp", "dev")
 F32 = jnp.float32
@@ -37,31 +38,27 @@
 
 
 def _units(lab, start, slot, blocks):
-    def visit(b, carry):
-        count, begin = carry
-        mesh = lab[b]
-        before = lab[jnp.maximum(b - 1, 0)]
-        opens = jnp.logical_or(jnp.logical_or(b == 0, mesh != before), b - begin == UNIT)
-        opens = jnp.logical_and(opens, mesh < MESHES)
-
-        @pl.when(opens)
-        def _():
-            start[count] = b
-            slot[count] = mesh - lab[0]
-
-        return count + opens.astype(jnp.int32), jnp.where(opens, b, begin)
-
+    count = jnp.int32(0)
+    begin = jnp.int32(0)
     used = jnp.int32(0)
     for b in range(blocks):
-        used = used + (lab[b] < MESHES).astype(jnp.int32)
-    count, _ = lax.fori_loop(0, blocks, visit, (jnp.int32(0), jnp.int32(0)))
+        mesh = lab[b]
+        in_use = mesh < MESHES
+        opens = b - begin == UNIT
+        opens = jnp.logical_or(opens, mesh != lab[b - 1]) if b else jnp.bool_(True)
+        opens = jnp.logical_and(opens, in_use)
+        start[count] = b
+        slot[count] = mesh - lab[0]
+        begin = jnp.where(opens, b, begin)
+        count = count + opens.astype(jnp.int32)
+        used = used + in_use.astype(jnp.int32)
     return count, used
 
 
 def gather_kernel(
-    lab, tal, sharp, x_hbm, gain_hbm, emb_hbm, pin_hbm, score_hbm,
+    lab_hbm, tal_hbm, sharp_hbm, x_hbm, gain_hbm, emb_hbm, pin_hbm, score_hbm,
     x_ref, w_ref, acc_ref, send_ref, start, slot, meta,
-    gain_ref, emb_ref, pin_ref, score_ref, wt_ref, st_ref, mean_ref, f_ref, sems, param_sems,
+    lab, tal, sharp, gain_ref, emb_ref, pin_ref, score_ref, wt_ref, st_ref, mean_ref, f_ref, sems, param_sems,
 ):
     blocks, block, width = x_hbm.shape
     points = UNIT * block
@@ -76,7 +73,15 @@
         part = pl.ds(i * PIECE, PIECE)
         return pltpu.make_async_copy(x_hbm.at[part], x_ref.at[part], sems.at[i])
 
-    given = ((gain_hbm, gain_ref), (emb_hbm, emb_ref), (pin_hbm, pin_ref), (score_hbm, score_ref))
+    given = (
+        (lab_hbm, lab),
+        (tal_hbm, tal),
+        (sharp_hbm, sharp),
+        (gain_hbm, gain_ref),
+        (emb_hbm, emb_ref),
+        (pin_hbm, pin_ref),
+        (score_hbm, score_ref),
+    )
     params = [pltpu.make_async_copy(a, b, param_sems.at[n]) for n, (a, b) in enumerate(given)]
     for p in params:
         p.start()
@@ -85,6 +90,8 @@
     row = lax.broadcasted_iota(jnp.int32, (width, width), 0)
     col = lax.broadcasted_iota(jnp.int32, (width, width), 1)
     mean_ref[...] = ((row == col).astype(F32) - 1.0 / width).astype(BF16)
+    for p in params[:3]:
+        p.wait()
     count, used = _units(lab, start, slot, blocks)
     start[count] = used
     for n in range(BATCH):
@@ -95,7 +102,7 @@
     meta[2] = used
     last = jnp.where(used > 0, slot[jnp.maximum(count - 1, 0)], 0)
     meta[3] = last
-    for p in params:
+    for p in params[3:]:
         p.wait()
     gain_ref[...] = gain_ref[...] * width**0.5
     wt_ref[:width, :] = emb_ref[...].astype(F32).T.astype(BF16)
@@ -133,33 +140,52 @@
         for b in range(UNIT):
             ref[s + b, row : row + value.shape[0], :] = value[:, b * block : (b + 1) * block]
 
-    for i in range(pieces):
-        copy(i).wait()
-
-    trips = (used + BATCH * UNIT - 1) // (BATCH * UNIT)
+    stride = WIDE * UNIT
+    trips = (used + stride - 1) // stride
 
     @pl.loop(0, trips)
     def _(j):
-        first = [(j * BATCH + n) * UNIT for n in range(BATCH)]
-        centres = [normalize(s) for s in first]
-        normed = [scale(c) for c in centres]
-        both = [_dot(wt_ref[...], n, ((1,), (1,))).astype(BF16) for n in normed]
-        for s, a in zip(first, both):
-            put(f_ref, s, 0, a[:width])
-        lives = [living(s) for s in first]
-        items = [(h, n) for h in range(heads) for n in range(BATCH)]
-        ahead = {}
-        for at in range(len(items) + BATCH):
-            if at < len(items):
-                h, n = items[at]
-                mid = both[n][width + h * dh : width + (h + 1) * dh, :]
-                ahead[h, n] = _dot(st_ref[h], jnp.concatenate([mid, mid, mid], axis=0), ((1,), (0,)))
-            if at >= BATCH:
-                h, n = items[at - BATCH]
-                put(w_ref, first[n], h * parts, weigh(ahead.pop((h, n)), lives[n]))
+        for i in range(stride // PIECE):
+            copy(j * (stride // PIECE) + i).wait()
+        first = [j * stride + n * UNIT for n in range(WIDE)]
+        centres, normed, both = {}, {}, {}
+
+        def project(pair):
+            def embed(n):
+                both[n] = _dot(wt_ref[...], normed.pop(n), ((1,), (1,))).astype(BF16)
+                put(f_ref, first[n], 0, both[n][:width])
+
+            steps = [lambda n=n: centres.__setitem__(n, normalize(first[n])) for n in pair]
+            steps += [lambda n=n: normed.__setitem__(n, scale(centres.pop(n))) for n in pair]
+            return steps + [lambda n=n: embed(n) for n in pair]
+
+        pairs = [(n, n + 1) for n in range(0, WIDE, 2)]
+        for step in project(pairs[0]):
+            step()
+        for at, pair in enumerate(pairs):
+            coming = project(pairs[at + 1]) if at + 1 < len(pairs) else []
+            lives = {n: living(first[n]) for n in pair}
+            items = [(h, n) for h in range(heads) for n in pair]
+            due = [int(0.8 * k * (len(items) + 2) / max(1, len(coming))) for k in range(len(coming))]
+            ahead = {}
+            for k in range(len(items) + 2):
+                if k < len(items):
+                    h, n = items[k]
+                    mid = both[n][width + h * dh : width + (h + 1) * dh, :]
+                    ahead[h, n] = _dot(st_ref[h], jnp.concatenate([mid, mid, mid], axis=0), ((1,), (0,)))
+                for step, when in zip(coming, due):
+                    if when == k:
+                        step()
+                if k >= 2:
+                    h, n = items[k - 2]
+                    put(w_ref, first[n], h * parts, weigh(ahead.pop((h, n)), lives[n]))
+
+    @pl.loop(trips * (stride // PIECE), pieces)
+    def _(i):
+        copy(i).wait()
 
     for b in range(UNIT):
-        w_ref[trips * BATCH * UNIT + b] = jnp.zeros(w_ref.shape[1:], BF16)
+        w_ref[trips * stride + b] = jnp.zeros(w_ref.shape[1:], BF16)
 
     def product(n, g):
         s = start[n]
@@ -370,7 +396,7 @@
     x, shares, sums, send, start, slot, meta = pl.pallas_call(
         gather_kernel,
         name="gather",
-        in_specs=[smem, smem, smem, hbm, hbm, hbm, hbm, hbm],
+        in_specs=[hbm] * 8,
         out_specs=[vmem, vmem, vmem, vmem, smem, smem, smem],
         out_shape=[
             pltpu.VMEM((room, block, width), BF16),
@@ -382,6 +408,9 @@
             jax.ShapeDtypeStruct((8,), jnp.int32),
         ],
         scratch_shapes=[
+            pltpu.SMEM((slots,), jnp.int32),
+            pltpu.SMEM((slots,), jnp.int32),
+            pltpu.SMEM((heads,), F32),
             pltpu.VMEM((1, width), F32),
             pltpu.VMEM((width, width), BF16),
             pltpu.VMEM((width, width), BF16),
@@ -391,7 +420,7 @@
             pltpu.VMEM((width, width), BF16),
             pltpu.VMEM((room, width, block), BF16),
             pltpu.SemaphoreType.DMA((pieces,)),
-            pltpu.SemaphoreType.DMA((4,)),
+            pltpu.SemaphoreType.DMA((7,)),
         ],
         compiler_params=params,
     )(

time: 62.6 us -> 60.2 us (0.962); the launches traced: 61.7 us -> 60.1 us
  Pallas kernels: 23.6 us -> 22 us
    pallas_call x1, Pallas kernels: 17 us -> 15.3 us  [on_device(): pl.pallas_call(gather_kernel, name='gather', in_specs=[hbm] * 8, out_spec...]
where the time goes in v3:
time: 60.2 us; the launch traced here: 60.1 us
  blocking collectives  37.5 us (62%)
  Pallas kernels  22 us (37%)
    all_to_all x1, blocking collectives, on_device(): got = lax.all_to_all(send, AXES, 0, 0, tiled=True)  23.5 us
    pallas_call x1, Pallas kernels, on_device(): pl.pallas_call(gather_kernel, name='gather', in_specs=[hbm] * 8, out_spec...  15.3 us
    all_to_all x1, blocking collectives, on_device(): tokens = lax.all_to_all(back, AXES, 0, 0, tiled=True)  14 us
    pallas_call x1, Pallas kernels, on_device(): pl.pallas_call(spread_kernel, name='spread', in_specs=[smem, smem, smem,...  6.08 us

profile of v3, /device:TPU:1, one launch (start us, length us, event | category | flops | bytes accessed | tf_op | source)
XLA Modules:
  0.0 60.1 jit_solution(12513531363417923722)
XLA Ops:
  0.0 0.0 copy-start.2
  0.0 0.0 copy-start
  0.0 0.0 copy-start.1
  0.0 15.3 %gather.1 = (bf16[68,128,256]{2,1,0:T(8,128)(2,1)S(1)}, bf16[68,512,128]{2,1,0:T(8,128)(2,1)S(1)}, f32[34,40,512]{2,1,0:T(8,128)S(1)}, f32[128,640]{1,0:T(8,128)...) custom-call(s32[64]{0:T(128)} %lab_hbm.1, s32[64]{0:T(128)} %tal.1, f32[8]{0:T(128)} %sharp_hbm.1, ...), custom_call_target="tpu_custom_call" | custom-call | tf_op jit(solution)/shard_map/gather/pallas_call | solution.py:396
  15.4 0.3 copy.11
  15.7 23.5 %all_to_all.22 = f32[128,1,640]{2,1,0:T(1,128)S(1)} all-to-all(f32[128,1,640]{2,1,0:T(1,128)S(1)} %copy.11), channel_id=1, replica_groups=mesh['grp'=8,'dev'=16] {'grp','dev'}, dimensions={0} | all-to-all | bytes 655360 | tf_op jit(solution)/shard_map/all_to_all | solution.py:436
  39.2 0.6 owner.1
  39.8 0.1 copy.12
  39.9 14.0 %all_to_all.23 = f32[128,1,256]{2,1,0:T(1,128)S(1)} all-to-all(f32[128,1,256]{2,1,0:T(1,128)S(1)} %copy.12), channel_id=1, replica_groups=mesh['grp'=8,'dev'=16] {'grp','dev'}, dimensions={0} | all-to-all | bytes 262144 | tf_op jit(solution)/shard_map/all_to_all | solution.py:443
  53.9 0.0 copy-done.2
  53.9 0.0 copy-done
  54.0 0.0 copy-done.1
  54.0 6.1 %spread.1 = bf16[64,128,256]{2,1,0:T(8,128)(2,1)} custom-call(s32[64]{0:T(128)S(1)} %copy-done.2, s32[128]{0:T(128)S(1)} %get-tuple-element.12.start, s32[128]{0:T(128)S(1)} %get-tuple-element.13.slot, s32[8]{0:T(128)S(1)} %get-tuple-element.14.meta, bf16[68,128,256]{2,1,0:T(8,128)(2,1)S(1)} %get-tuple-element.15.x_ref, ...), custom_call_target="tpu_custom_call" | custom-call | tf_op jit(solution)/shard_map/spread/pallas_call | solution.py:445
  (2 shorter events, 0.0 us)
Async XLA Ops:
  0.0 53.9 %copy-start.2 = (s32[64]{0:T(128)S(1)}, s32[64]{0:T(128)}, u32[]{:S(2)}) copy-start(s32[64]{0:T(128)} %tal.1) | copy-start | bytes 772
  0.0 53.9 %copy-start = (bf16[256,256]{1,0:T(8,128)(2,1)S(1)}, bf16[256,256]{1,0:T(8,128)(2,1)}, u32[]{:S(2)}) copy-start(bf16[256,256]{1,0:T(8,128)(2,1)} %out_proj_ref.1) | copy-start | bytes 393220
  0.0 54.0 %copy-start.1 = (f32[3,32,32]{2,1,0:T(8,128)S(1)}, f32[3,32,32]{2,1,0:T(8,128)}, u32[]{:S(2)}) copy-start(f32[3,32,32]{2,1,0:T(8,128)} %maps_ref.1) | copy-start | bytes 36868

commit v4 on v3

--- a/solution.py
+++ b/solution.py
@@ -189,13 +189,14 @@
 
     def product(n, g):
         s = start[n]
-        f = []
+        rows = slice(g * group * parts, (g + 1) * group * parts)
+        total = None
         for b in range(UNIT):
             part = jnp.concatenate([f_ref[s + b, g * group_points : (g + 1) * group_points], ones], axis=0)
-            f.append(jnp.where(s + b < start[n + 1], part, jnp.zeros_like(part)))
-        rows = slice(g * group * parts, (g + 1) * group * parts)
-        w = jnp.concatenate([w_ref[s + b, rows] for b in range(UNIT)], axis=1)
-        return _dot(jnp.concatenate(f, axis=1), w, ((1,), (1,)))
+            part = jnp.where(s + b < start[n + 1], part, jnp.zeros_like(part))
+            one = _dot(part, w_ref[s + b, rows], ((1,), (1,)))
+            total = one if total is None else total + one
+        return total
 
     @pl.loop(0, (count + BATCH - 1) // BATCH)
     def _(j):

time: 60.2 us -> 60.6 us (level); the launches traced: 60.1 us -> 59.7 us
  no operation moved by 1% of the time
where the time goes in v4:
time: 60.6 us; the launch traced here: 59.7 us
  blocking collectives  37.3 us (62%)
  Pallas kernels  21.8 us (36%)
    all_to_all x1, blocking collectives, on_device(): got = lax.all_to_all(send, AXES, 0, 0, tiled=True)  23.3 us
    pallas_call x1, Pallas kernels, on_device(): pl.pallas_call(gather_kernel, name='gather', in_specs=[hbm] * 8, out_spec...  15.1 us
    all_to_all x1, blocking collectives, on_device(): tokens = lax.all_to_all(back, AXES, 0, 0, tiled=True)  14 us
    pallas_call x1, Pallas kernels, on_device(): pl.pallas_call(spread_kernel, name='spread', in_specs=[smem, smem, smem,...  6.08 us

profile of v4, /device:TPU:1, one launch (start us, length us, event | category | flops | bytes accessed | tf_op | source)
XLA Modules:
  0.0 59.7 jit_solution(9282363742925133784)
XLA Ops:
  0.0 0.0 copy-start.2
  0.0 0.0 copy-start
  0.0 0.0 copy-start.1
  0.0 15.1 %gather.1 = (bf16[68,128,256]{2,1,0:T(8,128)(2,1)S(1)}, bf16[68,512,128]{2,1,0:T(8,128)(2,1)S(1)}, f32[34,40,512]{2,1,0:T(8,128)S(1)}, f32[128,640]{1,0:T(8,128)...) custom-call(s32[64]{0:T(128)} %lab_hbm.1, s32[64]{0:T(128)} %tal.1, f32[8]{0:T(128)} %sharp_hbm.1, ...), custom_call_target="tpu_custom_call" | custom-call | tf_op jit(solution)/shard_map/gather/pallas_call | solution.py:397
  15.2 0.3 copy.11
  15.5 23.3 %all_to_all.22 = f32[128,1,640]{2,1,0:T(1,128)S(1)} all-to-all(f32[128,1,640]{2,1,0:T(1,128)S(1)} %copy.11), channel_id=1, replica_groups=mesh['grp'=8,'dev'=16] {'grp','dev'}, dimensions={0} | all-to-all | bytes 655360 | tf_op jit(solution)/shard_map/all_to_all | solution.py:437
  38.9 0.6 owner.1
  39.4 0.1 copy.12
  39.6 14.0 %all_to_all.23 = f32[128,1,256]{2,1,0:T(1,128)S(1)} all-to-all(f32[128,1,256]{2,1,0:T(1,128)S(1)} %copy.12), channel_id=1, replica_groups=mesh['grp'=8,'dev'=16] {'grp','dev'}, dimensions={0} | all-to-all | bytes 262144 | tf_op jit(solution)/shard_map/all_to_all | solution.py:444
  53.6 0.0 copy-done.2
  53.6 0.0 copy-done
  53.6 0.0 copy-done.1
  53.6 6.1 %spread.1 = bf16[64,128,256]{2,1,0:T(8,128)(2,1)} custom-call(s32[64]{0:T(128)S(1)} %copy-done.2, s32[128]{0:T(128)S(1)} %get-tuple-element.12.start, s32[128]{0:T(128)S(1)} %get-tuple-element.13.slot, s32[8]{0:T(128)S(1)} %get-tuple-element.14.meta, bf16[68,128,256]{2,1,0:T(8,128)(2,1)S(1)} %get-tuple-element.15.x_ref, ...), custom_call_target="tpu_custom_call" | custom-call | tf_op jit(solution)/shard_map/spread/pallas_call | solution.py:446
  (2 shorter events, 0.0 us)
Async XLA Ops:
  0.0 53.6 %copy-start.2 = (s32[64]{0:T(128)S(1)}, s32[64]{0:T(128)}, u32[]{:S(2)}) copy-start(s32[64]{0:T(128)} %tal.1) | copy-start | bytes 772
  0.0 53.6 %copy-start = (bf16[256,256]{1,0:T(8,128)(2,1)S(1)}, bf16[256,256]{1,0:T(8,128)(2,1)}, u32[]{:S(2)}) copy-start(bf16[256,256]{1,0:T(8,128)(2,1)} %out_proj_ref.1) | copy-start | bytes 393220
  0.0 53.6 %copy-start.1 = (f32[3,32,32]{2,1,0:T(8,128)S(1)}, f32[3,32,32]{2,1,0:T(8,128)}, u32[]{:S(2)}) copy-start(f32[3,32,32]{2,1,0:T(8,128)} %maps_ref.1) | copy-start | bytes 36868
